TPU v7x, 32 devices: a whole 2x2x4 slice. The times are simulated.
32 devices in a mesh: role: 2 (over core), dev: 16 (over z, y, x).
Axes of the slice: x: 2, y: 2, z: 4, core: 2. Of those that a mesh axis runs over, the one named last changes fastest.
Arguments:
- table_rows: bfloat16 [32, 2048, 128], P('dev'), may hold values from -6 to 6
- piece_table: int32 [32], replicated, may hold values from 0 to 25, as said below
- bag_rows: int32 [32, 8192], P('dev'), may hold values from 0 to 2047
- bag_of: int32 [32, 8192], P('dev'), may hold values from 0 to 4095, never falling along the last dimension, each value on 1 to 8 neighbouring positions
- bag_weight: bfloat16 [32, 8192], P('dev'), may hold values from 0.25 to 2
- dense_input: bfloat16 [4096, 128], P('dev'), may hold values from -6 to 6
- labels: float32 [4096], P('dev'), may hold values from 0 to 1
- cross_u: bfloat16 [3456, 512], replicated, may hold values from -0.109375 to 0.109375
- cross_v: bfloat16 [512, 3456], replicated, may hold values from -0.25 to 0.25
- cross_bias: float32 [3456], replicated, may hold values from -3 to 3
- top_w1: bfloat16 [3456, 1024], replicated, may hold values from -0.109375 to 0.109375
- top_b1: float32 [1024], replicated, may hold values from -3 to 3
- out_w: bfloat16 [1024], replicated, may hold values from -0.375 to 0.375
Outputs:
- piece_grads: bfloat16 [16, 256, 32, 128], P(None, 'role', 'dev')
Inputs may be any that keep to these rules, and one draw needn't show every extreme that they name: `piece_table`: every one of the 26 tables owns one piece or more. `bag_of`: in each piece the bag numbers never fall along the lookups, and every sample has 1 to 8 lookups in every piece.
All inputs are finite; a program needn't handle non-finite values.
Results may differ from a plain program's by a relative error of at most 0.012.
The roundings to bfloat16 on the way count: a program that leaves them out, or rounds other values in their place, can miss the bound.
Values may be sent and summed in bfloat16 or wider, within the bound.
A program may use at most 128 MiB of HBM per device.

v0:
```python
import jax
import jax.numpy as jnp
from jax import lax
from jax.sharding import PartitionSpec as P


def as_sent(x):

    def short(part):
        return part.astype(jnp.bfloat16) if part.dtype == jnp.float32 else part

    return jax.tree.map(short, x)


def passed_along(value, axis, steps):
    count = lax.axis_size(axis)
    leading, last = (max(0, -steps), min(count, count - steps))
    return lax.ppermute(value, axis, [(source, source + steps) for source in range(leading, last)])


def dense_grads(pooled, dense_in, label_rows, cross_u, cross_v, cross_bias, top_w1, top_b1, out_w):
    row_count = pooled.shape[0]
    embed_width = dense_in.shape[1]
    features = jnp.concatenate([dense_in.astype(jnp.float32)[:, None, :], pooled], axis=1).reshape(
        row_count, -1
    )
    low_rank = jnp.dot(
        features.astype(jnp.bfloat16), cross_u, preferred_element_type=jnp.float32
    ).astype(jnp.bfloat16)
    cross_out = jnp.dot(low_rank, cross_v, preferred_element_type=jnp.float32) + cross_bias
    mixed = (features * cross_out + features).astype(jnp.bfloat16)
    pre_act = jnp.dot(mixed, top_w1, preferred_element_type=jnp.float32) + top_b1
    out_weight = out_w.astype(jnp.float32)
    sig_act = jax.nn.sigmoid(pre_act)
    logits = jnp.sum(pre_act * sig_act * out_weight, axis=1)
    grad_logit = jax.nn.sigmoid(logits) - label_rows
    slope = sig_act * (1.0 + pre_act * (1.0 - sig_act))
    grad_act = (grad_logit[:, None] * out_weight * slope).astype(jnp.bfloat16)
    grad_mixed = jnp.dot(grad_act, top_w1.T, preferred_element_type=jnp.float32)
    grad_cross = (grad_mixed * features).astype(jnp.bfloat16)
    grad_low = jnp.dot(grad_cross, cross_v.T, preferred_element_type=jnp.float32).astype(
        jnp.bfloat16
    )
    grad_features = grad_mixed * (cross_out + 1.0) + jnp.dot(
        grad_low, cross_u.T, preferred_element_type=jnp.float32
    )
    return grad_features.reshape(row_count, -1, embed_width)[:, 1:, :].astype(jnp.bfloat16)


def pool_pieces(
    table_rows, bag_rows, bag_of, bag_weight, offset, row_count, per_block, block_count
):
    local_pieces, piece_length, embed_width = table_rows.shape
    results = []
    for local_slot in range(local_pieces):
        bag_ids = bag_of[local_slot]
        within = bag_ids % per_block - offset
        chosen = (within >= 0) & (within < row_count)
        segment = jnp.where(chosen, bag_ids // per_block * row_count + within, 0)
        lookup_scale = jnp.where(chosen, bag_weight[local_slot].astype(jnp.float32), 0.0)
        picked = table_rows[local_slot][bag_rows[local_slot]]
        partial_sum = jax.ops.segment_sum(
            picked.astype(jnp.float32) * lookup_scale[:, None],
            segment,
            num_segments=block_count * row_count,
        )
        results.append(partial_sum.astype(jnp.bfloat16))
    stacked = jnp.stack(results, axis=1)
    return stacked.reshape(block_count, row_count, local_pieces, embed_width)


def dense_side(
    arrived,
    piece_table,
    table_count,
    dense_rows,
    label_rows,
    cross_u,
    cross_v,
    cross_bias,
    top_w1,
    top_b1,
    out_w,
):
    one_hot = (piece_table[None, :] == jnp.arange(table_count, dtype=jnp.int32)[:, None]).astype(
        jnp.bfloat16
    )
    pooled = jnp.einsum("rpe,tp->rte", arrived, one_hot, preferred_element_type=jnp.float32)
    grad_pooled = dense_grads(
        pooled, dense_rows, label_rows, cross_u, cross_v, cross_bias, top_w1, top_b1, out_w
    )
    return jnp.take(grad_pooled, piece_table, axis=1)[None]


def local(
    table_rows,
    piece_table,
    bag_rows,
    bag_of,
    bag_weight,
    dense_input,
    labels,
    cross_u,
    cross_v,
    cross_bias,
    top_w1,
    top_b1,
    out_w,
):
    devices = lax.axis_size("dev")
    role_index = lax.axis_index("role")
    per_block = dense_input.shape[0]
    half_rows = per_block // 2
    table_count = cross_bias.shape[0] // dense_input.shape[1] - 1
    local_pieces, piece_length, embed_width = table_rows.shape
    all_pieces = piece_table.shape[0]
    pooled_blocks = lax.cond(
        role_index == 0,
        lambda: pool_pieces(
            table_rows, bag_rows, bag_of, bag_weight, 0, per_block, per_block, devices
        ),
        lambda: jnp.zeros((devices, per_block, local_pieces, embed_width), jnp.bfloat16),
    )
    outgoing = lax.all_to_all(
        as_sent(pooled_blocks), "dev", split_axis=0, concat_axis=2, tiled=True
    ).astype(pooled_blocks.dtype)
    arrived = passed_along(as_sent(outgoing), "role", 1).astype(outgoing.dtype)
    gradients = lax.cond(
        role_index == 1,
        lambda: dense_side(
            arrived[0],
            piece_table,
            table_count,
            dense_input,
            labels,
            cross_u,
            cross_v,
            cross_bias,
            top_w1,
            top_b1,
            out_w,
        ),
        lambda: jnp.zeros((1, per_block, all_pieces, embed_width), jnp.bfloat16),
    )
    returned = lax.all_to_all(gradients, "dev", split_axis=2, concat_axis=0, tiled=True)
    upper_half = returned[:, half_rows:]
    lower_half = passed_along(returned[:, :half_rows], "role", -1)
    return jnp.where(role_index == 0, lower_half, upper_half)


def solution(mesh):
    return jax.shard_map(
        local,
        mesh=mesh,
        in_specs=(
            P("dev", None, None),
            P(),
            P("dev", None),
            P("dev", None),
            P("dev", None),
            P("dev", None),
            P("dev"),
            P(),
            P(),
            P(),
            P(),
            P(),
            P(),
        ),
        out_specs=P(None, "role", "dev", None),
        check_vma=False,
    )
```

profile of v0, /device:TPU:0, one launch (start us, length us, event | category | flops | bytes accessed | tf_op | source)
XLA Modules:
  0.0 310.2 jit_solution(1041741716662812616)
XLA Ops:
  0.0 179.2 %conditional.2 = (bf16[16,256,2,128]{3,1,0,2:T(8,128)(2,1)S(1)}) conditional(s32[]{:T(128)} %convert_element_type.63, () %tuple.18, (s32[2,8192]{1,0:T(2,128)}, bf16[2,2048,128]{2,1,0:T(8,128)(2,1)}, s32[2,8192]{1,0:T(2,128)}, bf16[2,8192]{1,0:T(2,128)(2,1)}) %tuple.19), branch_computations={%region_0.0_spmd, %region_1.4_spmd} | conditional | flops 9125888 | bytes 18776080 | solution.py:117
  0.0 1.6 compare_select_fusion.2
  1.6 1.0 fusion.39
  2.6 0.9 slice_convert_fusion.1
  3.5 2.1 slice_bitcast_fusion.1
  5.5 73.3 %scatter_custom_fusion = f32[4096,128]{1,0:T(8,128)S(1)} fusion(s32[8192]{0:T(1024)S(1)} %bitcast.93, f32[8192]{0:T(1024)S(1)} %and_select_fusion.7, f32[]{:T(128)} %constant.65.clone, bf16[2048,128]{1,0:T(8,128)(2,1)S(1)} %get-tuple-element.81, s32[8192]{0:T(1024)S(1)} %broadcast_clamp_fusion.1), kind=kCustom, calls=%fused_computation.40 | custom fusion | flops 3145728 | bytes 2686980 | tf_op jit(solution)/shard_map/cond/branch_1_fun/scatter-add | solution.py:62
  78.8 0.1 convert_element_type.48
  79.0 99.9 %scatter_custom_fusion.1 = f32[4096,128]{1,0:T(8,128)S(1)} fusion(s32[8192]{0:T(1024)S(1)} %bitcast.92, f32[8192]{0:T(1024)S(1)} %and_select_fusion.6, f32[]{:T(128)} %constant.65.clone, bf16[2048,128]{1,0:T(8,128)(2,1)} %get-tuple-element.82, s32[8192]{0:T(1024)S(1)} %broadcast_clamp_fusion), kind=kCustom, calls=%fused_computation.37 | custom fusion | flops 3145728 | bytes 2686980 | tf_op jit(solution)/shard_map/cond/branch_1_fun/scatter-add | solution.py:62
  178.9 0.1 convert_element_type.52
  179.0 0.2 pad_maximum_fusion.1
  179.2 0.1 copy.42
  179.4 0.0 copy-start.1
  179.4 0.0 copy-start.2
  179.4 0.0 copy-start.5
  179.4 36.1 %all_to_all.36 = bf16[16,256,2,128]{3,1,2,0:T(8,128)(2,1)S(1)} all-to-all(bf16[16,256,2,128]{3,1,2,0:T(8,128)(2,1)S(1)} %copy.42), channel_id=1, replica_groups=mesh['role'=2,'dev'=16] {'dev'}, dimensions={0} | all-to-all | bytes 4194304 | tf_op jit(solution)/shard_map/all_to_all | solution.py:124
  215.5 2.7 copy.43
  218.2 1.4 collective-permute-start
  219.6 3.8 %collective-permute-done = bf16[1,256,32,128]{3,2,1,0:T(8,128)(2,1)S(1)} collective-permute-done((bf16[1,256,32,128]{3,2,1,0:T(8,128)(2,1)}, bf16[1,256,32,128]{3,2,1,0:T(8,128)(2,1)S(1)}, u32[]{:S(2)}, u32[]{:S(2)}) %collective-permute-start) | collective-permute-done | bytes 2097184 | tf_op jit(solution)/shard_map/ppermute | solution.py:18
  223.5 0.0 copy-done.1
  223.5 0.0 copy-done.2
  223.5 0.0 copy-done.5
  223.5 0.7 conditional.3
  223.5 0.5 broadcast.324
  224.2 31.6 %all_to_all.37 = bf16[1,256,32,128]{3,1,0,2:T(8,128)(2,1)S(1)} all-to-all(bf16[1,256,32,128]{3,1,0,2:T(8,128)(2,1)S(1)} %bitcast.81), channel_id=1, replica_groups=mesh['role'=2,'dev'=16] {'dev'}, dimensions={2} | all-to-all | bytes 4194304 | tf_op jit(solution)/shard_map/all_to_all | solution.py:145
  255.7 0.1 slice.43
  255.8 1.3 collective-permute-start.1
  257.1 50.9 %collective-permute-done.1 = bf16[16,128,2,128]{3,1,2,0:T(8,128)(2,1)S(1)} collective-permute-done((bf16[16,128,2,128]{3,1,2,0:T(8,128)(2,1)S(1)}, bf16[16,128,2,128]{3,1,2,0:T(8,128)(2,1)S(1)}, u32[]{:S(2)}, u32[]{:S(2)}) %collective-permute-start.1) | collective-permute-done | bytes 1048608 | tf_op jit(solution)/shard_map/ppermute | solution.py:18
  308.0 0.1 slice_select_fusion
  308.1 2.1 copy.45
  (4 shorter events, 0.1 us)
Async XLA Ops:
  179.4 44.1 %copy-start.1 = (bf16[256,128]{1,0:T(8,128)(2,1)S(1)}, bf16[256,128]{1,0:T(8,128)(2,1)}, u32[]{:S(2)}) copy-start(bf16[256,128]{1,0:T(8,128)(2,1)} %param.22) | copy-start | bytes 196612
  179.4 44.1 %copy-start.2 = (f32[3456]{0:T(1024)S(1)}, f32[3456]{0:T(1024)}, u32[]{:S(2)}) copy-start(f32[3456]{0:T(1024)} %param.26) | copy-start | bytes 41476
  179.4 44.1 %copy-start.5 = (s32[32]{0:T(128)S(1)}, s32[32]{0:T(128)}, u32[]{:S(2)}) copy-start(s32[32]{0:T(128)} %param.18) | copy-start | bytes 388
  218.2 5.3 %collective-permute-start = (bf16[1,256,32,128]{3,2,1,0:T(8,128)(2,1)}, bf16[1,256,32,128]{3,2,1,0:T(8,128)(2,1)S(1)}, u32[]{:S(2)}, u32[]{:S(2)}) collective-permute-start(bf16[1,256,32,128]{3,2,1,0:T(8,128)(2,1)} %copy.43), channel_id=1, source_target_pairs={{0,16},{1,17},{2,18},{3,19},{4,20},{5,21},{6,22},{7,23},{8,24},{9,... | collective-permute-start | bytes 6291464 | tf_op jit(solution)/shard_map/ppermute | solution.py:18
  255.8 52.2 %collective-permute-start.1 = (bf16[16,128,2,128]{3,1,2,0:T(8,128)(2,1)S(1)}, bf16[16,128,2,128]{3,1,2,0:T(8,128)(2,1)S(1)}, u32[]{:S(2)}, u32[]{:S(2)}) collective-permute-start(bf16[16,128,2,128]{3,1,2,0:T(8,128)(2,1)S(1)} %slice.43), channel_id=1, source_target_pairs={{16,0},{17,1},{18,2},{19,3},{20,4},{21,5},{22,6},{23,7},{24,8},{25... | collective-permute-start | bytes 3145736 | tf_op jit(solution)/shard_map/ppermute | solution.py:18
where the time goes:
time: 311 us; the launch traced here: 310 us
  other arithmetic  176 us (57%)
  blocking collectives  67.7 us (22%)
  waiting for transfers between devices  54.7 us (18%)
  local copies, waits for them, and re-layouts  8.5 us (3%)
    scatter-add x2, other arithmetic, pool_pieces(): jax.ops.segment_sum(picked.astype(jnp.float32) * lookup_scale[:, None], s...  173 us
    ppermute x2, waiting for transfers between devices, passed_along(): lax.ppermute(value, axis, [(source, source + steps) for source in range(l...  54.7 us
    all_to_all x1, blocking collectives, local(): lax.all_to_all(as_sent(pooled_blocks), 'dev', split_axis=0, concat_axis=2...  36.1 us
    all_to_all x1, blocking collectives, local(): lax.all_to_all(gradients, 'dev', split_axis=2, concat_axis=0, tiled=True)  31.6 us
  transfers between devices with their start and end apart: 2, of which 2 were waited for; matrix products, arithmetic and copies ran while one was open for 0% of the time, Pallas kernels for 0%

commit v1 on v0

v1 whole, which is shorter than its diff:
```python
import functools

import jax
import jax.numpy as jnp
from jax import lax
from jax.experimental import pallas as pl
from jax.experimental.pallas import tpu as pltpu
from jax.sharding import PartitionSpec as P

LANES = 128
WINDOW = 256
LOW = 256
NT = (((1,), (1,)), ((), ()))
NN = (((1,), (0,)), ((), ()))


def dot(a, b, dims=NN):
    return lax.dot_general(a, b, dims, preferred_element_type=jnp.float32)


def pool_kernel(first_ref, last_ref, table_ref, rows_ref, bags_ref, scale_ref, out_ref, flipped, scale_wide):
    blocks, pieces, half, width = out_ref.shape
    length = table_ref.shape[1]
    total = rows_ref.shape[1]
    groups = length // LOW
    role = lax.axis_index("role")
    scale_wide[...] = scale_ref[...].astype(jnp.float32)
    for p in range(pieces):
        for g in range(groups):
            flipped[p, g * width : (g + 1) * width, :] = (
                table_ref[p, g * LOW : (g + 1) * LOW, :].astype(jnp.float32).T.astype(jnp.bfloat16)
            )
    low_ids = lax.broadcasted_iota(jnp.int32, (LOW, WINDOW), 0)
    bag_ids = lax.broadcasted_iota(jnp.int32, (half, WINDOW), 0)
    places = lax.broadcasted_iota(jnp.int32, (1, WINDOW), 1)

    def window(p, base, begin, first_bag):
        start = pl.multiple_of(jnp.minimum(begin, total - WINDOW), LANES)
        span = pl.ds(start, WINDOW)
        ids = rows_ref[pl.ds(p, 1), span]
        bags = bags_ref[pl.ds(p, 1), span] - first_bag
        bags = jnp.where(places + start >= begin, bags, -1)
        scale = scale_wide[pl.ds(p, 1), span]
        low, high = ids % LOW, ids // LOW
        hot = jnp.where(low_ids == low, 1.0, 0.0).astype(jnp.bfloat16)
        candidates = dot(flipped[p], hot)
        picked = candidates[:width]
        for g in range(1, groups):
            picked = jnp.where(high == g, candidates[g * width : (g + 1) * width], picked)
        spread = jnp.where(bag_ids == bags, scale, 0.0).astype(jnp.bfloat16)
        return dot(spread, picked.astype(jnp.bfloat16), NT)

    for p in range(pieces):

        @pl.loop(0, blocks)
        def _(k):
            first_bag = (2 * k + role) * half
            base = first_ref[p, k] // LANES * LANES
            count = (last_ref[p, k] - base + WINDOW - 1) // WINDOW

            def more(j, acc):
                return acc + window(p, base, base + j * WINDOW, first_bag)

            acc = window(p, base, base, first_bag)
            acc = lax.fori_loop(1, count, more, acc)
            out_ref[k, p] = acc.astype(jnp.bfloat16)


def pool(table_rows, bag_rows, bag_of, bag_weight, half, blocks):
    pieces, length, width = table_rows.shape
    role = lax.axis_index("role")
    edges = (2 * jnp.arange(blocks, dtype=jnp.int32) + role) * half
    first = jnp.sum((bag_of[:, None, :] < edges[None, :, None]).astype(jnp.int32), axis=2)
    last = jnp.sum((bag_of[:, None, :] < edges[None, :, None] + half).astype(jnp.int32), axis=2)
    vmem = pl.BlockSpec(memory_space=pltpu.VMEM)
    smem = pl.BlockSpec(memory_space=pltpu.SMEM)
    return pl.pallas_call(
        pool_kernel,
        out_shape=jax.ShapeDtypeStruct((blocks, pieces, half, width), jnp.bfloat16),
        in_specs=[smem, smem, vmem, vmem, vmem, vmem],
        out_specs=vmem,
        scratch_shapes=[
            pltpu.VMEM((pieces, length // LOW * width, LOW), jnp.bfloat16),
            pltpu.VMEM(bag_weight.shape, jnp.float32),
        ],
        compiler_params=pltpu.CompilerParams(vmem_limit_bytes=40 * 1024 * 1024),
    )(first, last, table_rows, bag_rows, bag_of, bag_weight)


def dense_kernel(
    owner_ref, arrived_ref, dense_ref, label_ref, bias_ref, b1_ref, out_w_ref, u_hbm, v_hbm, w_hbm,
    out_ref, u_ref, v_ref, w_ref, feats, crossed, mixed_grad, grads, sems,
):
    pieces, rows, width = arrived_ref.shape
    wide = feats.shape[1]
    role = lax.axis_index("role")
    load_u = pltpu.make_async_copy(u_hbm, u_ref, sems.at[0])
    load_v = pltpu.make_async_copy(v_hbm, v_ref, sems.at[1])
    load_w = pltpu.make_async_copy(w_hbm, w_ref, sems.at[2])
    load_u.start()
    load_v.start()
    load_w.start()

    feats[...] = jnp.zeros_like(feats)
    feats[:, :width] = dense_ref[pl.ds(pl.multiple_of(role * rows, rows), rows), :].astype(jnp.float32)

    @pl.loop(0, pieces)
    def _(p):
        at = pl.ds(pl.multiple_of((owner_ref[p] + 1) * width, width), width)
        feats[:, at] = feats[:, at] + arrived_ref[p].astype(jnp.float32)

    step = next(n for n in (3 * width, width) if wide % n == 0)
    parts = [slice(i, i + step) for i in range(0, wide, step)]

    load_u.wait()
    low_rank = dot(feats[...].astype(jnp.bfloat16), u_ref[...]).astype(jnp.bfloat16)
    load_v.wait()
    load_w.wait()
    pre_act = b1_ref[...]
    for part in parts:
        cross_out = dot(low_rank, v_ref[:, part]) + bias_ref[:, part]
        crossed[:, part] = cross_out
        own = feats[:, part]
        pre_act = pre_act + dot((own * cross_out + own).astype(jnp.bfloat16), w_ref[part, :])
    out_weight = out_w_ref[...].astype(jnp.float32)
    sig_act = jax.nn.sigmoid(pre_act)
    logits = jnp.sum(pre_act * sig_act * out_weight, axis=1, keepdims=True)
    row_at = lax.broadcasted_iota(jnp.int32, (rows, rows), 0)
    column_at = lax.broadcasted_iota(jnp.int32, (rows, rows), 1)
    labels = jnp.sum(
        jnp.where(row_at == column_at, label_ref[pl.ds(role, 1), :], 0.0), axis=1, keepdims=True
    )
    grad_logit = jax.nn.sigmoid(logits) - labels
    slope = sig_act * (1.0 + pre_act * (1.0 - sig_act))
    grad_act = (grad_logit * out_weight * slope).astype(jnp.bfloat16)
    grad_low = jnp.zeros((rows, u_ref.shape[1]), jnp.float32)
    for part in parts:
        grad_mixed = dot(grad_act, w_ref[part, :], NT)
        grad_cross = (grad_mixed * feats[:, part]).astype(jnp.bfloat16)
        mixed_grad[:, part] = grad_mixed * (crossed[:, part] + 1.0)
        grad_low = grad_low + dot(grad_cross, v_ref[:, part], NT)
    grad_low = grad_low.astype(jnp.bfloat16)
    for part in parts:
        total = (mixed_grad[:, part] + dot(grad_low, u_ref[part, :], NT)).astype(jnp.bfloat16)
        for i in range(step // width):
            grads[part.start // width + i] = total[:, i * width : (i + 1) * width]

    @pl.loop(0, pieces)
    def _(p):
        out_ref[p] = grads[owner_ref[p] + 1]


def dense(arrived, piece_table, dense_input, labels, cross_u, cross_v, cross_bias, top_w1, top_b1, out_w):
    pieces, rows, width = arrived.shape
    wide, rank = cross_u.shape
    hidden = top_w1.shape[1]
    vmem = pl.BlockSpec(memory_space=pltpu.VMEM)
    smem = pl.BlockSpec(memory_space=pltpu.SMEM)
    anywhere = pl.BlockSpec(memory_space=pl.ANY)
    return pl.pallas_call(
        dense_kernel,
        out_shape=jax.ShapeDtypeStruct(arrived.shape, jnp.bfloat16),
        in_specs=[smem] + [vmem] * 6 + [anywhere] * 3,
        out_specs=vmem,
        scratch_shapes=[
            pltpu.VMEM(cross_u.shape, jnp.bfloat16),
            pltpu.VMEM(cross_v.shape, jnp.bfloat16),
            pltpu.VMEM(top_w1.shape, jnp.bfloat16),
            pltpu.VMEM((rows, wide), jnp.float32),
            pltpu.VMEM((rows, wide), jnp.float32),
            pltpu.VMEM((rows, wide), jnp.float32),
            pltpu.VMEM((wide // width, rows, width), jnp.bfloat16),
            pltpu.SemaphoreType.DMA((3,)),
        ],
        compiler_params=pltpu.CompilerParams(vmem_limit_bytes=56 * 1024 * 1024),
    )(
        piece_table, arrived, dense_input, labels.reshape(2, rows), cross_bias[None], top_b1[None],
        out_w[None], cross_u, cross_v, top_w1,
    )


def local(
    table_rows, piece_table, bag_rows, bag_of, bag_weight, dense_input, labels,
    cross_u, cross_v, cross_bias, top_w1, top_b1, out_w,
):
    devices = lax.axis_size("dev")
    half = dense_input.shape[0] // 2
    pieces, _, width = table_rows.shape
    pooled = pool(table_rows, bag_rows, bag_of, bag_weight, half, devices)
    arrived = lax.all_to_all(pooled, "dev", split_axis=0, concat_axis=0, tiled=True)
    arrived = arrived.reshape(devices * pieces, half, width)
    grads = dense(
        arrived, piece_table, dense_input, labels, cross_u, cross_v, cross_bias, top_w1, top_b1, out_w
    )
    grads = grads.reshape(devices, pieces, half, width)
    returned = lax.all_to_all(grads, "dev", split_axis=0, concat_axis=0, tiled=True)
    return returned.transpose(0, 2, 1, 3)


def solution(mesh):
    split, whole = P("dev"), P()
    return jax.shard_map(
        local,
        mesh=mesh,
        in_specs=(split, whole, split, split, split, split, split) + (whole,) * 6,
        out_specs=P(None, "role", "dev", None),
        check_vma=False,
    )
```

time: 311 us -> 122 us (0.39)
  other arithmetic: 176 us -> 1.28 us
  Pallas kernels: 0 us -> 48.1 us
  blocking collectives: 67.7 us -> 32.6 us
  waiting for transfers between devices: 54.7 us -> 24 us
  starting transfers between devices: 2.7 us -> 7.96 us
    scatter-add x2 -> x0, other arithmetic: 173 us -> none  [pool_pieces(): jax.ops.segment_sum(picked.astype(jnp.float32) * lookup_scale[:, None], s...]
    ppermute x2 -> x0, waiting for transfers between devices: 54.7 us -> none  [passed_along(): lax.ppermute(value, axis, [(source, source + steps) for source in range(l...]
    pallas_call x0 -> x2, Pallas kernels: none -> 48.1 us  [the longest x1 32.2 us: pool(): pl.pallas_call(pool_kernel, out_shape=jax.ShapeDtypeStruct((blocks, piece...]
    all_to_all x2 -> x1, blocking collectives: 67.7 us -> 32.6 us  [local(): lax.all_to_all(grads, 'dev', split_axis=0, concat_axis=0, tiled=True)]
    all_to_all x0 -> x1, waiting for transfers between devices: none -> 24 us  [local(): lax.all_to_all(pooled, 'dev', split_axis=0, concat_axis=0, tiled=True)]
    all_to_all x0 -> x1, starting transfers between devices: none -> 7.96 us  [local(): lax.all_to_all(pooled, 'dev', split_axis=0, concat_axis=0, tiled=True)]
    unnamed x6 -> x15, local copies, waits for them, and re-layouts: 0.02 us -> 5.6 us
  transfers between devices with their start and end apart: 2 -> 1, of which waited for: 2 -> 1; matrix products, arithmetic and copies ran while one was open for 0% -> 1% of each run, Pallas kernels for 0% -> 0%
where the time goes in v1:
time: 122 us; the launch traced here: 123 us
  Pallas kernels  48.1 us (39%)
  blocking collectives  32.6 us (27%)
  waiting for transfers between devices  24 us (20%)
  local copies, waits for them, and re-layouts  9.12 us (7%)
  starting transfers between devices  7.96 us (7%)
  other arithmetic  1.28 us (1%)
    all_to_all x1, blocking collectives, local(): lax.all_to_all(grads, 'dev', split_axis=0, concat_axis=0, tiled=True)  32.6 us
    pallas_call x1, Pallas kernels, pool(): pl.pallas_call(pool_kernel, out_shape=jax.ShapeDtypeStruct((blocks, piece...  32.2 us
    all_to_all x1, waiting for transfers between devices, local(): lax.all_to_all(pooled, 'dev', split_axis=0, concat_axis=0, tiled=True)  24 us
    pallas_call x1, Pallas kernels, dense(): pl.pallas_call(dense_kernel, out_shape=jax.ShapeDtypeStruct(arrived.shape...  15.9 us
    all_to_all x1, starting transfers between devices, local(): lax.all_to_all(pooled, 'dev', split_axis=0, concat_axis=0, tiled=True)  7.96 us
    unnamed x15, local copies, waits for them, and re-layouts  5.6 us
  transfers between devices with their start and end apart: 1, of which 1 were waited for; matrix products, arithmetic and copies ran while one was open for 1% of the time, Pallas kernels for 0%

profile of v1, /device:TPU:0, one launch (start us, length us, event | category | flops | bytes accessed | tf_op | source)
XLA Modules:
  0.0 123.1 jit_solution(2763903592379143678)
XLA Ops:
  0.0 0.0 copy-start.5
  0.0 0.0 copy-start.6
  0.0 1.3 %convert_reduce_fusion = (s32[2,16]{1,0:T(2,128)S(1)}, s32[2,16]{1,0:T(2,128)S(1)}) fusion(s32[2,8192]{1,0:T(2,128)} %bags_ref.1, s32[16]{0:T(128)S(1)} %get-tuple-element.8, s32[16]{0:T(128)S(1)} %get-tuple-element.7), kind=kLoop, calls=%fused_computation | loop fusion | flops 1572800 | bytes 65920 | tf_op jit(solution)/shard_map/reduce_sum | solution.py:74
  1.3 0.0 copy-start
  1.3 1.2 copy-done
  2.5 0.0 copy-start.1
  2.5 0.8 copy-done.1
  3.4 0.0 copy-start.2
  3.4 0.8 copy-done.2
  4.2 0.0 copy-start.3
  4.2 0.8 copy-done.3
  4.9 32.2 %shard_map.127 = bf16[16,2,128,128]{3,2,1,0:T(8,128)(2,1)} custom-call(s32[2,16]{1,0:T(2,128)S(1)} %get-tuple-element.6.first_ref, s32[2,16]{1,0:T(2,128)S(1)} %get-tuple-element.5.last_ref, bf16[2,2048,128]{2,1,0:T(8,128)(2,1)S(1)} %copy-done, s32[2,8192]{1,0:T(2,128)S(1)} %copy-done.2, s32[2,8192]{1,0:T(2,128)S(1)} %copy-done.1, bf16[2,8192]{1,0:T(2,128)(2,1)S(1)} %copy-done.3), custom_call_target="tpu_custom_call" | custom-call | tf_op jit(solution)/shard_map/pallas_call | solution.py:77
  37.2 8.0 %all-to-all-start = ((bf16[16,2,128,128]{3,2,1,0:T(8,128)(2,1)}), bf16[16,2,128,128]{3,2,1,0:T(8,128)(2,1)S(1)}, u32[]{:S(2)}, u32[]{:S(2)}) async-start(bf16[16,2,128,128]{3,2,1,0:T(8,128)(2,1)} %shard_map.127), calls=%async_computation | async-start | bytes 2097152 | tf_op jit(solution)/shard_map/all_to_all | solution.py:190
  45.1 0.0 copy-done.5
  45.1 0.6 broadcast_in_dim.6.bias_ref
  45.7 0.0 copy-done.6
  45.8 0.6 broadcast_in_dim.15.out_w_ref
  46.3 24.0 %all-to-all-done = bf16[16,2,128,128]{3,2,1,0:T(8,128)(2,1)S(1)} async-done(((bf16[16,2,128,128]{3,2,1,0:T(8,128)(2,1)}), bf16[16,2,128,128]{3,2,1,0:T(8,128)(2,1)S(1)}, u32[]{:S(2)}, u32[]{:S(2)}) %all-to-all-start) | async-done | bytes 1048608 | tf_op jit(solution)/shard_map/all_to_all | solution.py:190
  70.4 0.0 copy-start.4
  70.4 1.0 copy-done.4
  71.3 15.9 %shard_map.128 = bf16[32,128,128]{2,1,0:T(8,128)(2,1)} custom-call(s32[32]{0:T(128)} %owner_ref.1, bf16[32,128,128]{2,1,0:T(8,128)(2,1)} %bitcast.5, bf16[256,128]{1,0:T(8,128)(2,1)} %dense_ref.1, f32[2,128]{1,0:T(2,128)} %bitcast.9, f32[1,3456]{1,0:T(1,128)} %broadcast_in_dim.6.bias_ref, f32[1,1024]{1,0:T(1,128)} %bitcast.8, ...), custom_call_target="tpu_custom_call" | custom-call | tf_op jit(solution)/shard_map/pallas_call | solution.py:160
  87.2 2.3 %copy.15 = bf16[16,2,128,128]{3,1,2,0:T(2,128)(2,1)S(1)} copy(bf16[16,2,128,128]{3,2,1,0:T(8,128)(2,1)} %bitcast.6) | data formatting | bytes 2097152 | tf_op jit(solution)/shard_map/reshape | solution.py:195
  89.5 32.6 %all_to_all.10 = bf16[16,2,128,128]{3,1,2,0:T(2,128)(2,1)S(1)} all-to-all(bf16[16,2,128,128]{3,1,2,0:T(2,128)(2,1)S(1)} %copy.15), channel_id=1, replica_groups=mesh['role'=2,'dev'=16] {'dev'}, dimensions={0} | all-to-all | bytes 2097152 | tf_op jit(solution)/shard_map/all_to_all | solution.py:196
  122.1 1.0 copy.17
  (1 shorter events, 0.0 us)
Async XLA Ops:
  0.0 45.1 %copy-start.5 = (f32[3456]{0:T(1024)S(1)}, f32[3456]{0:T(1024)}, u32[]{:S(2)}) copy-start(f32[3456]{0:T(1024)} %param.22) | copy-start | bytes 41476
  0.0 45.7 %copy-start.6 = (bf16[1024]{0:T(1024)(128)(2,1)S(1)}, bf16[1024]{0:T(1024)(128)(2,1)}, u32[]{:S(2)}) copy-start(bf16[1024]{0:T(1024)(128)(2,1)} %param.25) | copy-start | bytes 6148
  1.3 1.2 copy-start
  2.5 0.8 copy-start.1
  3.4 0.8 copy-start.2
  4.2 0.8 copy-start.3
  37.2 33.2 %all-to-all-start = ((bf16[16,2,128,128]{3,2,1,0:T(8,128)(2,1)}), bf16[16,2,128,128]{3,2,1,0:T(8,128)(2,1)S(1)}, u32[]{:S(2)}, u32[]{:S(2)}) async-start(bf16[16,2,128,128]{3,2,1,0:T(8,128)(2,1)} %shard_map.127), calls=%async_computation | async-start | bytes 2097152 | tf_op jit(solution)/shard_map/all_to_all | solution.py:190
  70.4 1.0 copy-start.4
